TPU v7x, 32 devices: a whole 2x2x4 slice. The times are simulated.
32 devices in a mesh: grp: 2 (over y), col: 4 (over z), row: 2 (over x), dir: 2 (over core).
Axes of the slice: x: 2, y: 2, z: 4, core: 2. Of those that a mesh axis runs over, the one named last changes fastest.
Arguments:
- slopes_in: bfloat16 [512, 8192], P(None, ('grp', 'col')), parts along dimension 1, may hold values from -6 to 6
- basis_left: bfloat16 [12, 16, 256, 256], P(('row', 'dir'), 'col'), may hold values from -0.09375 to 0.09375
- basis_right: bfloat16 [12, 16, 256, 256], P(('row', 'dir'), 'col'), may hold values from -0.375 to 0.375
- rank_blocks: int32 [12, 16], P(('row', 'dir'), 'col'), may hold values from 1 to 4
- tile_owner: int32 [16], replicated, may hold values from 0 to 15, each once
- footprint: int32 [4, 4, 4, 2048], P(('row', 'dir')), may hold values from 0 to 767
- trace_weight: float32 [4, 4, 4, 2048], P(('row', 'dir')), may hold values from 0 to 0.5
- fitting: bfloat16 [2048, 4096], P(None, 'col'), may hold values from -0.125 to 0.125
Outputs:
- commands: bfloat16 [4, 1024, 4096], P(('row', 'dir'), 'grp', 'col'), parts along dimension 1
There are 2 independent parts, one for each index of `grp`. A program takes and returns all parts, laid end to end along the dimension named above; an argument that names none is the same for every part. Nothing has to cross between parts.
Inputs may be any that keep to these rules, and one draw needn't show every extreme that they name: rank_blocks[i, k] is the number of leading blocks of 64 columns of tile (i, k) that are live. `tile_owner`: each slope block appears in exactly one tile slot. `footprint`: indices into one layer's points.
All inputs are finite; a program needn't handle non-finite values.
Results may differ from a plain program's by a relative error of at most 0.0064.
Values may be sent and summed in bfloat16 or wider, within the bound.
No kernel may reach another device: no remote copies, remote signals or barrier semaphores. Data moves between devices by JAX's collectives and lax.ppermute only.
A program may use at most 128 MiB of HBM per device.

v0:
```python
import jax
import jax.numpy as jnp
from jax import lax
from jax.sharding import PartitionSpec as P

RB = 64


def shards(
    slopes_in, basis_left, basis_right, rank_blocks, tile_owner, footprint, trace_weight, fitting
):
    frames = slopes_in.shape[0]
    tile_size = basis_left.shape[2]
    rows_here = basis_left.shape[0]
    slots_here = basis_left.shape[1]
    rank_cols = basis_left.shape[3]
    owners = lax.dynamic_slice_in_dim(tile_owner, lax.axis_index("col") * slots_here, slots_here, 0)
    share = frames // lax.axis_size(("row", "dir"))
    mine = lax.dynamic_slice_in_dim(slopes_in, lax.axis_index(("row", "dir")) * share, share, 0)
    partial_value = lax.all_gather(mine, "col", axis=1, tiled=True)
    picked = jnp.take(partial_value.reshape(share, -1, tile_size), owners, axis=1)
    chosen = lax.all_gather(picked, ("row", "dir"), axis=0, tiled=True)
    columns = jnp.arange(rank_cols, dtype=jnp.int32) // RB
    live = columns[None, None, None, :] < rank_blocks[:, :, None, None]
    frame_share = frames // lax.axis_size("col")
    coeffs = jnp.einsum("fkn,iknr->ikfr", chosen, basis_right, preferred_element_type=jnp.float32)
    coeffs = jnp.where(live, coeffs, 0.0).astype(jnp.bfloat16)
    summed = jnp.einsum("ikfr,iknr->fin", coeffs, basis_left, preferred_element_type=jnp.float32)
    layer_block = lax.psum_scatter(
        summed.reshape(lax.axis_size("col") * frame_share, rows_here * tile_size),
        "col",
        scatter_dimension=0,
        tiled=True,
    ).astype(jnp.bfloat16)
    layers = lax.all_gather(layer_block, ("row", "dir"), axis=1, tiled=True)
    layer_count = footprint.shape[1]
    pupil_count = footprint.shape[3]
    per_layer = layers.shape[1] // layer_count
    shifts = (jnp.arange(layer_count, dtype=jnp.int32) * per_layer)[:, None, None]
    flat = (footprint[0] + shifts).reshape(-1)
    values = (
        jnp.take(layers, flat, axis=1)
        .astype(jnp.float32)
        .reshape(frame_share, layer_count, 4, pupil_count)
    )
    pupil = jnp.sum(values * trace_weight[0][None], axis=(1, 2)).astype(jnp.bfloat16)
    commands = jnp.dot(
        lax.all_gather(pupil, "col", axis=0, tiled=True),
        fitting,
        preferred_element_type=jnp.float32,
    )
    return commands.astype(jnp.bfloat16)[None]


def solution(mesh):
    placed = (
        P(None, ("grp", "col")),
        P(("row", "dir"), "col", None, None),
        P(("row", "dir"), "col", None, None),
        P(("row", "dir"), "col"),
        P(),
        P(("row", "dir"), None, None, None),
        P(("row", "dir"), None, None, None),
        P(None, "col"),
    )
    return jax.shard_map(
        shards,
        mesh=mesh,
        in_specs=placed,
        out_specs=P(("row", "dir"), "grp", "col"),
        check_vma=False,
    )
```

profile of v0, /device:TPU:0, one launch (start us, length us, event | category | flops | bytes accessed | tf_op | source)
XLA Modules:
  0.0 293.8 jit_solution(6185712206535708235)
XLA Ops:
  6.5 0.0 copy-start
  6.5 0.0 copy-start.1
  6.5 0.0 copy-start.3
  6.5 0.0 all-gather.4.cloned.1.call-start
  6.6 1.1 constant_dynamic-slice_fusion
  7.7 0.8 copy.14
  8.5 0.0 all-gather.4.cloned.1.call-update
  8.5 0.0 all-gather.6.cloned.1.call-start
  8.6 0.7 compare_and_fusion.1
  9.3 30.3 %all-gather.4.cloned.1.call-done = bf16[128,4096]{0,1:T(8,128)(2,1)} async-done(((bf16[128,1024]{0,1:T(8,128)(2,1)}), bf16[128,4096]{0,1:T(8,128)(2,1)}) %all-gather.4.cloned.1.call-update) | async-done | bytes 1048592 | tf_op jit(solution)/shard_map/all_gather | solution.py:20
  39.6 1.5 copy.12
  41.1 0.6 gather_fusion
  41.7 0.8 select_bitcast_fusion
  42.5 0.0 all-gather.6.cloned.1.call-update
  42.5 0.0 reduce-scatter.2.cloned.1.call-start
  42.6 0.1 add.67
  42.7 0.2 add.75
  42.9 0.0 copy-done.1
  42.9 0.2 squeeze.6
  43.1 0.0 copy-done.3
  43.1 0.1 broadcast_compare_fusion
  43.1 15.6 %all-gather.6.cloned.1.call-done = bf16[512,4,256]{2,0,1:T(8,128)(2,1)} async-done(((bf16[128,4,256]{2,0,1:T(8,128)(2,1)}), bf16[512,4,256]{2,0,1:T(8,128)(2,1)}) %all-gather.6.cloned.1.call-update) | async-done | bytes 1048592 | tf_op jit(solution)/shard_map/all_gather | solution.py:22
  58.8 0.0 copy-done
  58.8 4.7 %fusion.1 = f32[3,512,256,1]{1,2,3,0:T(8,128)} fusion(bf16[3,4,256,256]{3,2,1,0:T(8,128)(2,1)S(1)} %copy-done, pred[3,4,256]{2,1,0:T(4,128)(4,1)S(1)} %broadcast_compare_fusion, bf16[3,4,256,256]{3,2,1,0:T(8,128)(2,1)} %param.10, bf16[512,4,256]{2,0,1:T(8,128)(2,1)} %all-gather.6.cloned.1.call-done), kind=kOutput, calls=%fused_computation.5 | convolution fusion | flops 1613758464 | bytes 5770240 | tf_op jit(solution)/shard_map/ikfr,iknr->fin/dot_general | solution.py:28
  63.4 0.0 reduce-scatter.2.cloned.1.call-update
  63.5 0.0 all-gather.8.cloned.1.call-start
  63.5 0.2 compare_select_fusion
  63.7 0.2 compare_and_fusion
  63.9 35.2 %reduce-scatter.2.cloned.1.call-done = f32[128,768]{0,1:T(8,128)} async-done(((f32[512,768]{0,1:T(8,128)}), f32[128,768]{0,1:T(8,128)}) %reduce-scatter.2.cloned.1.call-update) | async-done | bytes 393232 | tf_op jit(solution)/shard_map/reduce_scatter | solution.py:29
  99.1 1.0 convert_element_type.17
  100.1 8.6 %all_gather.14 = bf16[128,3072]{0,1:T(8,128)(2,1)S(1)} all-gather(bf16[128,768]{0,1:T(8,128)(2,1)S(1)} %convert_element_type.17), channel_id=1, replica_groups=mesh['grp'=2,'col'=4,'row'=2,'dir'=2] {'row','dir'}, dimensions={1}, use_global_device_ids=true | all-gather | bytes 983040 | tf_op jit(solution)/shard_map/all_gather | solution.py:35
  108.6 0.0 copy-start.2
  108.6 114.3 %gather_fusion.1 = bf16[32768,128]{1,0:T(8,128)(2,1)} fusion(bf16[128,3072]{0,1:T(8,128)(2,1)S(1)} %all_gather.14, s32[32768]{0:T(1024)S(1)} %broadcast_clamp_fusion), kind=kCustom, calls=%fused_computation.1 | custom fusion | bytes 16908288 | tf_op jit(solution)/shard_map/jit(_take)/gather | solution.py:42
  222.9 0.0 copy-done.2
  222.9 13.4 %multiply_reduce_fusion = bf16[128,2048]{0,1:T(8,128)(2,1)} fusion(f32[4,4,2048]{2,1,0:T(4,128)S(1)} %bitcast.39, bf16[128,4,4,2048]{0,3,2,1:T(8,128)(2,1)} %bitcast.35, pred[4,4,2048]{2,1,0:T(4,128)(4,1)S(1)} %compare_and_fusion), kind=kLoop, calls=%fused_computation.2 | loop fusion | flops 16515072 | bytes 9076736 | tf_op jit(solution)/shard_map/reduce_sum | solution.py:46
  236.3 0.0 all-gather.8.cloned.1.call-update
  236.3 44.8 %all-gather.8.cloned.1.call-done = bf16[512,2048]{0,1:T(8,128)(2,1)} async-done(((bf16[128,2048]{0,1:T(8,128)(2,1)}), bf16[512,2048]{0,1:T(8,128)(2,1)}) %all-gather.8.cloned.1.call-update) | async-done | bytes 2097168 | tf_op jit(solution)/shard_map/all_gather | solution.py:48
  281.2 6.1 %fusion.7 = bf16[1,512,1024]{2,1,0:T(8,128)(2,1)} fusion(bf16[512,2048]{0,1:T(8,128)(2,1)} %all-gather.8.cloned.1.call-done, bf16[2048,1024]{1,0:T(8,128)(2,1)} %param.15), kind=kOutput, calls=%fused_computation.10 | convolution fusion | flops 2148007936 | bytes 7340032 | tf_op jit(solution)/shard_map/dot_general | solution.py:47
  (4 shorter events, 0.0 us)
Async XLA Ops:
  6.5 52.2 %copy-start = (bf16[3,4,256,256]{3,2,1,0:T(8,128)(2,1)S(1)}, bf16[3,4,256,256]{3,2,1,0:T(8,128)(2,1)}, u32[]{:S(2)}) copy-start(bf16[3,4,256,256]{3,2,1,0:T(8,128)(2,1)} %param.9) | copy-start | bytes 4718596
  6.5 36.3 %copy-start.1 = (s32[1,4,4,2048]{3,2,1,0:T(4,128)S(1)}, s32[1,4,4,2048]{3,2,1,0:T(4,128)}, u32[]{:S(2)}) copy-start(s32[1,4,4,2048]{3,2,1,0:T(4,128)} %param.13) | copy-start | bytes 393220
  6.5 36.5 %copy-start.3 = (s32[3,4]{1,0:T(4,128)S(1)}, s32[3,4]{1,0:T(4,128)}, u32[]{:S(2)}) copy-start(s32[3,4]{1,0:T(4,128)} %param.11) | copy-start | bytes 148
  6.5 33.1 %all-gather.4.cloned.1.call-start = ((), (), s32[]{:S(2)}) async-start(), calls=%async_computation.1 | async-start | bytes 1310720 | tf_op jit(solution)/shard_map/all_gather | solution.py:20
  8.5 50.2 %all-gather.6.cloned.1.call-start = ((), (), s32[]{:S(2)}) async-start(), calls=%async_computation.2 | async-start | bytes 1310720 | tf_op jit(solution)/shard_map/all_gather | solution.py:22
  42.5 56.5 %reduce-scatter.2.cloned.1.call-start = ((), (), s32[]{:S(2)}) async-start(), calls=%async_computation.3 | async-start | bytes 1966080 | tf_op jit(solution)/shard_map/reduce_scatter | solution.py:29
  63.5 217.7 %all-gather.8.cloned.1.call-start = ((), (), s32[]{:S(2)}) async-start(), calls=%async_computation.4 | async-start | bytes 2621440 | tf_op jit(solution)/shard_map/all_gather | solution.py:48
  108.6 114.3 %copy-start.2 = (f32[1,4,4,2048]{3,2,1,0:T(4,128)S(1)}, f32[1,4,4,2048]{3,2,1,0:T(4,128)}, u32[]{:S(2)}) copy-start(f32[1,4,4,2048]{3,2,1,0:T(4,128)} %param.14) | copy-start | bytes 393220
Sparse Core Ops, SparseCore 0:
  8.9 30.6 all-gather.3
  42.6 16.0 all-gather.5
  63.6 35.4 reduce-scatter.1
  236.5 44.6 all-gather.7
where the time goes:
time: 294 us
  waiting for transfers between devices  126 us (43%)
  local copies, waits for them, and re-layouts  119 us (40%)
  other arithmetic  16.4 us (6%)
  between operations  13.2 us (4%)
  matrix products  10.8 us (4%)
  blocking collectives  8.58 us (3%)
    gather x1, local copies, waits for them, and re-layouts, shards(): jnp.take(layers, flat, axis=1).astype(jnp.float32)  114 us
    all_gather x1, waiting for transfers between devices, shards(): lax.all_gather(pupil, 'col', axis=0, tiled=True)  44.8 us
    reduce_scatter x1, waiting for transfers between devices, shards(): lax.psum_scatter(summed.reshape(lax.axis_size('col') * frame_share, rows_...  35.2 us
    all_gather x1, waiting for transfers between devices, shards(): partial_value = lax.all_gather(mine, 'col', axis=1, tiled=True)  30.3 us
    all_gather x1, waiting for transfers between devices, shards(): chosen = lax.all_gather(picked, ('row', 'dir'), axis=0, tiled=True)  15.6 us
    reduce_sum x1, other arithmetic, shards(): jnp.sum(values * trace_weight[0][None], axis=(1, 2)).astype(jnp.bfloat16)  13.4 us
    all_gather x1, blocking collectives, shards(): layers = lax.all_gather(layer_block, ('row', 'dir'), axis=1, tiled=True)  8.58 us
    dot_general x1, matrix products, shards(): jnp.dot(lax.all_gather(pupil, 'col', axis=0, tiled=True), fitting, prefer...  6.14 us
  transfers between devices with their start and end apart: 4, of which 4 were waited for; matrix products, arithmetic and copies ran while one was open for 1% of the time, Pallas kernels for 0%

commit v1 on v0

--- a/solution.py
+++ b/solution.py
@@ -4,6 +4,12 @@
 from jax.sharding import PartitionSpec as P
 
 RB = 64
+
+
+def in_order(blocks, dim):
+    blocks = jnp.moveaxis(blocks, 0, dim)
+    shape = blocks.shape
+    return blocks.reshape(*shape[:dim], shape[dim] * shape[dim + 1], *shape[dim + 2 :])
 
 
 def shards(
@@ -19,11 +25,25 @@
     mine = lax.dynamic_slice_in_dim(slopes_in, lax.axis_index(("row", "dir")) * share, share, 0)
     partial_value = lax.all_gather(mine, "col", axis=1, tiled=True)
     picked = jnp.take(partial_value.reshape(share, -1, tile_size), owners, axis=1)
-    chosen = lax.all_gather(picked, ("row", "dir"), axis=0, tiled=True)
     columns = jnp.arange(rank_cols, dtype=jnp.int32) // RB
     live = columns[None, None, None, :] < rank_blocks[:, :, None, None]
     frame_share = frames // lax.axis_size("col")
-    coeffs = jnp.einsum("fkn,iknr->ikfr", chosen, basis_right, preferred_element_type=jnp.float32)
+    size, index, rows = (
+        lax.axis_size(("row", "dir")),
+        lax.axis_index(("row", "dir")),
+        picked.shape[0],
+    )
+    forward = [(i, (i + 1) % size) for i in range(size)]
+    blocks = []
+    carried = picked
+    for step in range(size):
+        following = carried if step == size - 1 else lax.ppermute(carried, ("row", "dir"), forward)
+        blocks.append(
+            jnp.einsum("fkn,iknr->ikfr", carried, basis_right, preferred_element_type=jnp.float32)
+        )
+        carried = following
+    blocks = jnp.stack(blocks)[(index - jnp.arange(size)) % size]
+    coeffs = in_order(blocks, 2)
     coeffs = jnp.where(live, coeffs, 0.0).astype(jnp.bfloat16)
     summed = jnp.einsum("ikfr,iknr->fin", coeffs, basis_left, preferred_element_type=jnp.float32)
     layer_block = lax.psum_scatter(

time: 294 us -> 302 us (1.027)
  local copies, waits for them, and re-layouts: 119 us -> 127 us
    all_gather x1 -> x0, waiting for transfers between devices: 15.6 us -> none  [shards(): chosen = lax.all_gather(picked, ('row', 'dir'), axis=0, tiled=True)]
    ppermute x0 -> x3, waiting for transfers between devices: none -> 15.6 us  [shards(): lax.ppermute(carried, ('row', 'dir'), forward)]
    gather x0 -> x1, local copies, waits for them, and re-layouts: none -> 4.31 us  [shards(): blocks = jnp.stack(blocks)[(index - jnp.arange(size)) % size]]
  transfers between devices with their start and end apart: 4 -> 6, of which waited for: 4 -> 6; matrix products, arithmetic and copies ran while one was open for 1% -> 1% of each run, Pallas kernels for 0% -> 0%
where the time goes in v1:
time: 302 us
  local copies, waits for them, and re-layouts  127 us (42%)
  waiting for transfers between devices  125 us (41%)
  other arithmetic  18.4 us (6%)
  between operations  13.3 us (4%)
  matrix products  9.88 us (3%)
  blocking collectives  8.58 us (3%)
    gather x1, local copies, waits for them, and re-layouts, shards(): jnp.take(layers, flat, axis=1).astype(jnp.float32)  115 us
    all_gather x1, waiting for transfers between devices, shards(): lax.all_gather(pupil, 'col', axis=0, tiled=True)  44.8 us
    reduce_scatter x1, waiting for transfers between devices, shards(): lax.psum_scatter(summed.reshape(lax.axis_size('col') * frame_share, rows_...  34.5 us
    all_gather x1, waiting for transfers between devices, shards(): partial_value = lax.all_gather(mine, 'col', axis=1, tiled=True)  30.3 us
    ppermute x3, waiting for transfers between devices, shards(): lax.ppermute(carried, ('row', 'dir'), forward)  15.6 us
    reduce_sum x1, other arithmetic, shards(): jnp.sum(values * trace_weight[0][None], axis=(1, 2)).astype(jnp.bfloat16)  13.4 us
    all_gather x1, blocking collectives, shards(): layers = lax.all_gather(layer_block, ('row', 'dir'), axis=1, tiled=True)  8.58 us
    dot_general x1, matrix products, shards(): jnp.dot(lax.all_gather(pupil, 'col', axis=0, tiled=True), fitting, prefer...  6.14 us
  transfers between devices with their start and end apart: 6, of which 6 were waited for; matrix products, arithmetic and copies ran while one was open for 1% of the time, Pallas kernels for 0%

profile of v1, /device:TPU:0, one launch (start us, length us, event | category | flops | bytes accessed | tf_op | source)
XLA Modules:
  0.0 302.1 jit_solution(14214362011150699467)
XLA Ops:
  6.5 0.0 copy-start
  6.5 0.0 all-gather.3.cloned.1.call-start
  6.6 1.1 constant_dynamic-slice_fusion
  7.7 0.8 copy.37
  8.5 0.0 all-gather.3.cloned.1.call-update
  8.5 0.0 reduce-scatter.2.cloned.1.call-start
  8.6 0.7 compare_and_fusion.1
  9.4 30.3 %all-gather.3.cloned.1.call-done = bf16[128,4096]{0,1:T(8,128)(2,1)} async-done(((bf16[128,1024]{0,1:T(8,128)(2,1)}), bf16[128,4096]{0,1:T(8,128)(2,1)}) %all-gather.3.cloned.1.call-update) | async-done | bytes 1048592 | tf_op jit(solution)/shard_map/all_gather | solution.py:26
  39.6 1.5 copy.26
  41.1 0.6 gather_fusion
  41.7 0.1 fusion.10
  41.8 0.1 collective-permute-start
  41.9 0.0 copy-done.4
  41.9 0.1 broadcast_compare_fusion
  42.0 5.7 %collective-permute-done = bf16[128,4,256]{2,0,1:T(8,128)(2,1)S(1)} collective-permute-done((bf16[128,4,256]{2,0,1:T(8,128)(2,1)S(1)}, bf16[128,4,256]{2,0,1:T(8,128)(2,1)S(1)}, u32[]{:S(2)}, u32[]{:S(2)}) %collective-permute-start) | collective-permute-done | bytes 262176 | tf_op jit(solution)/shard_map/ppermute | solution.py:40
  47.7 0.0 collective-permute-start.1
  47.7 0.1 add.91
  47.8 0.2 add.101
  47.9 0.0 copy-done.2
  47.9 0.2 squeeze.6
  48.1 0.0 copy-done
  48.1 0.4 convolution_bitcast_fusion.3
  48.5 4.9 %collective-permute-done.1 = bf16[128,4,256]{2,0,1:T(8,128)(2,1)S(1)} collective-permute-done((bf16[128,4,256]{2,0,1:T(8,128)(2,1)S(1)}, bf16[128,4,256]{2,0,1:T(8,128)(2,1)S(1)}, u32[]{:S(2)}, u32[]{:S(2)}) %collective-permute-start.1) | collective-permute-done | bytes 262176 | tf_op jit(solution)/shard_map/ppermute | solution.py:40
  53.5 0.0 collective-permute-start.2
  53.5 0.4 convolution_bitcast_fusion.2
  53.8 0.4 convolution_bitcast_fusion.1
  54.2 5.0 %collective-permute-done.2 = bf16[128,4,256]{2,0,1:T(8,128)(2,1)S(1)} collective-permute-done((bf16[128,4,256]{2,0,1:T(8,128)(2,1)S(1)}, bf16[128,4,256]{2,0,1:T(8,128)(2,1)S(1)}, u32[]{:S(2)}, u32[]{:S(2)}) %collective-permute-start.2) | collective-permute-done | bytes 262176 | tf_op jit(solution)/shard_map/ppermute | solution.py:40
  59.2 0.4 convolution_bitcast_fusion
  59.6 1.9 pad_maximum_fusion
  61.5 4.3 %gather_fusion.1 = bf16[4,3,4,128,256]{4,3,1,2,0:T(8,128)(2,1)} fusion(bf16[4,3,4,128,256]{4,3,1,2,0:T(8,128)(2,1)} %pad_maximum_fusion, s32[1024]{0:T(1024)S(1)} %pad_clamp_fusion), kind=kCustom, calls=%fused_computation.1 | custom fusion | bytes 6291472 | tf_op jit(solution)/shard_map/gather | solution.py:45
  65.8 2.2 copy.31
  68.0 0.0 copy-start.1
  68.1 0.8 fusion
  68.8 0.6 copy-done.1
  69.5 2.2 fusion.14
  71.6 0.0 reduce-scatter.2.cloned.1.call-update
  71.7 0.0 all-gather.5.cloned.1.call-start
  71.7 0.2 compare_select_fusion
  71.9 0.2 compare_and_fusion
  72.1 34.5 %reduce-scatter.2.cloned.1.call-done = f32[128,768]{0,1:T(8,128)} async-done(((f32[512,768]{0,1:T(8,128)}), f32[128,768]{0,1:T(8,128)}) %reduce-scatter.2.cloned.1.call-update) | async-done | bytes 393232 | tf_op jit(solution)/shard_map/reduce_scatter | solution.py:49
  106.6 1.0 convert_element_type.17
  107.6 8.6 %all_gather.10 = bf16[128,3072]{0,1:T(8,128)(2,1)S(1)} all-gather(bf16[128,768]{0,1:T(8,128)(2,1)S(1)} %convert_element_type.17), channel_id=1, replica_groups=mesh['grp'=2,'col'=4,'row'=2,'dir'=2] {'row','dir'}, dimensions={1}, use_global_device_ids=true | all-gather | bytes 983040 | tf_op jit(solution)/shard_map/all_gather | solution.py:55
  116.2 115.0 %gather_fusion.2 = bf16[32768,128]{1,0:T(8,128)(2,1)} fusion(bf16[128,3072]{0,1:T(8,128)(2,1)S(1)} %all_gather.10, s32[32768]{0:T(1024)S(1)} %broadcast_clamp_fusion), kind=kCustom, calls=%fused_computation.2 | custom fusion | bytes 16908288 | tf_op jit(solution)/shard_map/jit(_take)/gather | solution.py:62
  231.2 0.0 copy-done.3
  231.2 13.4 %multiply_reduce_fusion = bf16[128,2048]{0,1:T(8,128)(2,1)} fusion(f32[4,4,2048]{2,1,0:T(4,128)S(1)} %bitcast.75, bf16[128,4,4,2048]{0,3,2,1:T(8,128)(2,1)} %bitcast.70, pred[4,4,2048]{2,1,0:T(4,128)(4,1)S(1)} %compare_and_fusion), kind=kLoop, calls=%fused_computation.3 | loop fusion | flops 16515072 | bytes 9076736 | tf_op jit(solution)/shard_map/reduce_sum | solution.py:66
  244.6 0.0 all-gather.5.cloned.1.call-update
  244.6 44.8 %all-gather.5.cloned.1.call-done = bf16[512,2048]{0,1:T(8,128)(2,1)} async-done(((bf16[128,2048]{0,1:T(8,128)(2,1)}), bf16[512,2048]{0,1:T(8,128)(2,1)}) %all-gather.5.cloned.1.call-update) | async-done | bytes 2097168 | tf_op jit(solution)/shard_map/all_gather | solution.py:68
  289.5 6.1 %fusion.1 = bf16[1,512,1024]{2,1,0:T(8,128)(2,1)} fusion(bf16[512,2048]{0,1:T(8,128)(2,1)} %all-gather.5.cloned.1.call-done, bf16[2048,1024]{1,0:T(8,128)(2,1)} %param.15), kind=kOutput, calls=%fused_computation.12 | convolution fusion | flops 2148007936 | bytes 7340032 | tf_op jit(solution)/shard_map/dot_general | solution.py:67
  (9 shorter events, 0.1 us)
Async XLA Ops:
  6.5 41.6 %copy-start = (bf16[3,4,256,256]{3,2,1,0:T(8,128)(2,1)S(1)}, bf16[3,4,256,256]{3,2,1,0:T(8,128)(2,1)}, u32[]{:S(2)}) copy-start(bf16[3,4,256,256]{3,2,1,0:T(8,128)(2,1)} %param.10) | copy-start | bytes 4718596
  6.5 35.3 %copy-start.4 = (s32[3,4]{1,0:T(4,128)S(1)}, s32[3,4]{1,0:T(4,128)}, u32[]{:S(2)}) copy-start(s32[3,4]{1,0:T(4,128)} %param.11) | copy-start | bytes 148
  6.5 41.4 %copy-start.2 = (s32[1,4,4,2048]{3,2,1,0:T(4,128)S(1)}, s32[1,4,4,2048]{3,2,1,0:T(4,128)}, u32[]{:S(2)}) copy-start(s32[1,4,4,2048]{3,2,1,0:T(4,128)} %param.13) | copy-start | bytes 393220
  6.5 33.1 %all-gather.3.cloned.1.call-start = ((), (), s32[]{:S(2)}) async-start(), calls=%async_computation.1 | async-start | bytes 1310720 | tf_op jit(solution)/shard_map/all_gather | solution.py:26
  8.5 98.1 %reduce-scatter.2.cloned.1.call-start = ((), (), s32[]{:S(2)}) async-start(), calls=%async_computation.2 | async-start | bytes 1966080 | tf_op jit(solution)/shard_map/reduce_scatter | solution.py:49
  41.8 5.8 %collective-permute-start = (bf16[128,4,256]{2,0,1:T(8,128)(2,1)S(1)}, bf16[128,4,256]{2,0,1:T(8,128)(2,1)S(1)}, u32[]{:S(2)}, u32[]{:S(2)}) collective-permute-start(bf16[128,4,256]{2,0,1:T(8,128)(2,1)S(1)} %fusion.10), channel_id=1, source_target_pairs={{0,1},{1,2},{2,3},{3,0},{4,5},{5,6},{6,7},{7,4},{8,9},{9,10},{10,1... | collective-permute-start | bytes 786440 | tf_op jit(solution)/shard_map/ppermute | solution.py:40
  47.7 5.8 %collective-permute-start.1 = (bf16[128,4,256]{2,0,1:T(8,128)(2,1)S(1)}, bf16[128,4,256]{2,0,1:T(8,128)(2,1)S(1)}, u32[]{:S(2)}, u32[]{:S(2)}) collective-permute-start(bf16[128,4,256]{2,0,1:T(8,128)(2,1)S(1)} %collective-permute-done), channel_id=1, source_target_pairs={{0,1},{1,2},{2,3},{3,0},{4,5},{5,6},{6,7},{7,4},{8,9},{9,10},{10,1... | collective-permute-start | bytes 786440 | tf_op jit(solution)/shard_map/ppermute | solution.py:40
  53.5 5.8 %collective-permute-start.2 = (bf16[128,4,256]{2,0,1:T(8,128)(2,1)S(1)}, bf16[128,4,256]{2,0,1:T(8,128)(2,1)S(1)}, u32[]{:S(2)}, u32[]{:S(2)}) collective-permute-start(bf16[128,4,256]{2,0,1:T(8,128)(2,1)S(1)} %collective-permute-done.1), channel_id=1, source_target_pairs={{0,1},{1,2},{2,3},{3,0},{4,5},{5,6},{6,7},{7,4},{8,9},{9,10},{10,1... | collective-permute-start | bytes 786440 | tf_op jit(solution)/shard_map/ppermute | solution.py:40
  68.0 1.4 copy-start.1
  71.7 217.8 %all-gather.5.cloned.1.call-start = ((), (), s32[]{:S(2)}) async-start(), calls=%async_computation.3 | async-start | bytes 2621440 | tf_op jit(solution)/shard_map/all_gather | solution.py:68
  116.2 115.0 %copy-start.3 = (f32[1,4,4,2048]{3,2,1,0:T(4,128)S(1)}, f32[1,4,4,2048]{3,2,1,0:T(4,128)}, u32[]{:S(2)}) copy-start(f32[1,4,4,2048]{3,2,1,0:T(4,128)} %param.14) | copy-start | bytes 393220
Sparse Core Ops, SparseCore 0:
  8.9 30.6 all-gather.2
  71.8 34.8 reduce-scatter.1
  244.8 44.6 all-gather.4
